TPU v7x, 32 devices: a whole 2x2x4 slice. The times are simulated.
32 devices in a mesh: dp: 8 (over z, y), mp: 4 (over x, core).
Axes of the slice: x: 2, y: 2, z: 4, core: 2. Of those that a mesh axis runs over, the one named last changes fastest.
Arguments:
- streams: bfloat16 [2048, 4, 8192], P('dp', None, 'mp'), may hold values from -200 to 200
- branch_out: bfloat16 [2048, 8192], P('dp', 'mp'), may hold values from -6 to 6
- merge_weight: float32 [20, 4, 8192], P(None, None, ('mp', 'dp')), may hold values from -0.03125 to 0.03125
- next_weight: float32 [24, 4, 8192], P(None, None, ('mp', 'dp')), may hold values from -0.03125 to 0.03125
- blend_bias: float32 [44], replicated, may hold values from -3 to 3
- blend_scale: float32 [5], replicated, may hold values from 0.5 to 3
- norm_gain: float32 [8192], P('mp'), may hold values from 0.5 to 1.5
Outputs:
- streams_out: bfloat16 [2048, 4, 8192], P('dp', None, 'mp')
- branch_in: bfloat16 [2048, 8192], P('dp', 'mp')
- next_mix: float32 [2048, 20], P('dp')
All inputs are finite; a program needn't handle non-finite values.
Results may differ from a plain program's by a relative error of at most 0.001.
Values sent between devices are 32-bit elements; how exact they have to be, the bound alone decides.
No kernel may reach another device: no remote copies, remote signals or barrier semaphores. Data moves between devices by JAX's collectives and lax.ppermute only.
A program may use at most 64 MiB of HBM per device.

v0:
```python
import jax
import jax.numpy as jnp
from jax import lax
from jax.sharding import PartitionSpec as P

D = 8192
STREAMS = 4
BALANCE_ROUNDS = 6
epsilon = 1e-06


def balance_normalize(balanced_matrix):
    for balance_round in range(BALANCE_ROUNDS):
        balanced_matrix = balanced_matrix / jnp.sum(balanced_matrix, axis=2, keepdims=True)
        balanced_matrix = balanced_matrix / jnp.sum(balanced_matrix, axis=1, keepdims=True)
    return balanced_matrix


def settle(columns, finish):
    summed = lax.psum(columns, "mp")
    result = finish(summed)
    return result


def first_coef(raw_sums, squares, blend_bias, blend_scale):
    rms_root = jnp.sqrt(squares / (STREAMS * D) + epsilon)
    score_logits = raw_sums / rms_root[:, None]
    post_mix = 2.0 * jax.nn.sigmoid(blend_scale[0] * score_logits[:, :4] + blend_bias[:4])
    residual_blend = balance_normalize(
        jnp.exp(
            blend_scale[1] * score_logits[:, 4:20].reshape(-1, 4, 4)
            + blend_bias[4:20].reshape(4, 4)
        )
    )
    return (post_mix, residual_blend)


def second_coef(raw_sums, squares, blend_bias, blend_scale):
    rms_root = jnp.sqrt(squares / (STREAMS * D) + epsilon)
    score_logits = raw_sums / rms_root[:, None]
    pre_next = jax.nn.sigmoid(blend_scale[2] * score_logits[:, :4] + blend_bias[20:24])
    post_next = 2.0 * jax.nn.sigmoid(blend_scale[3] * score_logits[:, 4:8] + blend_bias[24:28])
    residual_following = balance_normalize(
        jnp.exp(
            blend_scale[4] * score_logits[:, 8:24].reshape(-1, 4, 4)
            + blend_bias[28:44].reshape(4, 4)
        )
    )
    return (pre_next, post_next, residual_following)


def mix_streams(residual_blend, post_mix, streams, branch_out):
    branch_wide = branch_out.astype(jnp.float32)
    outputs = []
    for target in range(STREAMS):
        total = post_mix[:, target, None] * branch_wide
        for source in range(STREAMS):
            total = total + residual_blend[:, target, source, None] * streams[:, source, :].astype(
                jnp.float32
            )
        outputs.append(total)
    return jnp.stack(outputs, axis=1)


def unite(pre_next, mixed):
    total = pre_next[:, 0, None] * mixed[:, 0, :]
    for source in range(1, STREAMS):
        total = total + pre_next[:, source, None] * mixed[:, source, :]
    return total


def local(streams, branch_out, merge_weight, next_weight, blend_bias, blend_scale, norm_gain):
    merge_rows, next_rows = (
        lax.all_gather(merge_weight, "dp", axis=2, tiled=True),
        lax.all_gather(next_weight, "dp", axis=2, tiled=True),
    )
    highest = lax.Precision.HIGHEST
    raw_part = jnp.einsum(
        "tic,kic->tk", streams, merge_rows, precision=highest, preferred_element_type=jnp.float32
    )
    gram_part = jnp.einsum("tic,tjc->tij", streams, streams, preferred_element_type=jnp.float32)
    columns = jnp.concatenate([raw_part, jnp.trace(gram_part, axis1=1, axis2=2)[:, None]], axis=1)

    def finish_first(summed):
        post_mix, residual_blend = first_coef(
            summed[:, :20], summed[:, 20], blend_bias, blend_scale
        )
        return jnp.concatenate([post_mix, residual_blend.reshape(-1, 16)], axis=1)

    merge_coef = settle(columns, finish_first)
    post_mix = merge_coef[:, :4]
    residual_blend = merge_coef[:, 4:20].reshape(-1, 4, 4)
    mixed = mix_streams(residual_blend, post_mix, streams, branch_out)
    streams_out = mixed.astype(jnp.bfloat16)
    raw_next = jnp.einsum("tic,kic->tk", mixed, next_rows, precision=highest)
    extra_cols = jnp.sum(mixed * mixed, axis=(1, 2))[:, None]
    columns_next = jnp.concatenate([raw_next, extra_cols], axis=1)

    def finish_second(summed):
        squares = summed[:, 24]
        pre_next, post_next, residual_following = second_coef(
            summed[:, :24], squares, blend_bias, blend_scale
        )
        pieces = [pre_next, post_next, residual_following.reshape(-1, 16)]
        return jnp.concatenate(pieces, axis=1)

    next_coef = settle(columns_next, finish_second)
    pre_next = next_coef[:, :4]
    next_mix = next_coef[:, 4:24]
    united = unite(pre_next, mixed)
    united_sq = lax.psum(jnp.sum(united * united, axis=1), "mp")
    branch_in = (united / jnp.sqrt(united_sq / D + epsilon)[:, None] * norm_gain).astype(
        jnp.bfloat16
    )
    return (streams_out, branch_in, next_mix)


def solution(mesh):
    placed = (
        P("dp", None, "mp"),
        P("dp", "mp"),
        P(None, None, ("mp", "dp")),
        P(None, None, ("mp", "dp")),
        P(),
        P(),
        P("mp"),
    )
    return jax.shard_map(
        local,
        mesh=mesh,
        in_specs=placed,
        out_specs=(P("dp", None, "mp"), P("dp", "mp"), P("dp", None)),
        check_vma=False,
    )
```

profile of v0, /device:TPU:0, one launch (start us, length us, event | category | flops | bytes accessed | tf_op | source)
XLA Modules:
  0.0 152.0 jit_solution(15976659351027897930)
XLA Ops:
  0.7 9.4 %fusion.28 = f32[256]{0:T(256)S(1)} fusion(bf16[256,4,2048]{2,1,0:T(4,128)(2,1)} %param.7, pred[4,4]{1,0:T(4,128)(4,1)S(1)} %iota_compare_fusion), kind=kOutput, calls=%fused_computation.54 | convolution fusion | flops 16785152 | bytes 4195344 | tf_op jit(solution)/shard_map/tic,tjc->tij/dot_general | solution.py:81
  10.2 0.1 add.136
  10.4 0.6 fusion.78
  11.1 33.9 %all_gather.7 = f32[24,4,2048]{2,0,1:T(8,128)S(1)} all-gather(f32[24,4,256]{2,0,1:T(8,128)S(1)} %copy.16), channel_id=1, replica_groups=mesh['dp'=8,'mp'=4] {'dp'}, dimensions={2}, use_global_device_ids=true | all-gather | bytes 884736 | tf_op jit(solution)/shard_map/all_gather | solution.py:75
  45.0 32.1 %all_gather.6 = f32[20,4,2048]{2,0,1:T(8,128)S(1)} all-gather(f32[20,4,256]{2,0,1:T(8,128)S(1)} %copy.10), channel_id=1, replica_groups=mesh['dp'=8,'mp'=4] {'dp'}, dimensions={2}, use_global_device_ids=true | all-gather | bytes 737280 | tf_op jit(solution)/shard_map/all_gather | solution.py:74
  77.1 9.2 %convolution_bitcast_fusion = f32[256,20]{0,1:T(8,128)S(1)} fusion(f32[20,4,2048]{2,0,1:T(8,128)S(1)} %all_gather.6, bf16[256,4,2048]{2,1,0:T(4,128)(2,1)} %param.7), kind=kOutput, calls=%fused_computation.56 | convolution fusion | flops 503316480 | bytes 4870144 | tf_op jit(solution)/shard_map/tic,kic->tk/dot_general | solution.py:78
  86.3 10.4 %psum.21 = f32[256,21]{0,1:T(8,128)S(1)} all-reduce(f32[256,21]{0,1:T(8,128)S(1)} %pad_maximum_fusion.5), channel_id=1, replica_groups=mesh['dp'=8,'mp'=4] {'mp'}, use_global_device_ids=true, to_apply=%region_1.2 | all-reduce | flops 5376 | bytes 43008 | tf_op jit(solution)/shard_map/psum | solution.py:20
  96.7 0.8 fusion.56
  97.5 0.7 slice_multiply_fusion.1
  98.2 0.1 fusion.74
  98.6 4.6 %copy.11 = bf16[256,4,2048]{2,0,1:T(8,128)(2,1)S(1)} copy(bf16[256,4,2048]{2,1,0:T(4,128)(2,1)} %param.7) | data formatting | bytes 8388608 | tf_op args[0]
  103.2 2.3 %fusion.13 = (f32[256,2048]{1,0:T(8,128)S(1)}, f32[256,2048]{1,0:T(8,128)S(1)}) fusion(bf16[256,2048]{1,0:T(8,128)(2,1)S(1)} %copy-done.4, f32[256]{0:T(256)S(1)} %bitcast.135, f32[256]{0:T(256)S(1)} %bitcast.136, f32[256]{0:T(256)S(1)} %bitcast.137, f32[256]{0:T(256)S(1)} %bitcast.130, f32[256]{0:T(256)S(1)} %bitcast.140, ...), kind=kLoop, calls=%fused_computation.35 | loop fusion | flops 12058624 | bytes 9447424 | tf_op jit(solution)/shard_map/add | solution.py:58
  105.5 2.3 %fusion.21 = (f32[256,2048]{1,0:T(8,128)S(1)}, f32[256,2048]{1,0:T(8,128)S(1)}) fusion(bf16[256,2048]{1,0:T(8,128)(2,1)S(1)} %copy-done.4, f32[256]{0:T(256)S(1)} %bitcast.126, f32[256]{0:T(256)S(1)} %bitcast.127, f32[256]{0:T(256)S(1)} %bitcast.128, f32[256]{0:T(256)S(1)} %bitcast.129, f32[256]{0:T(256)S(1)} %bitcast.139, ...), kind=kLoop, calls=%fused_computation.43 | loop fusion | flops 12058624 | bytes 9447424 | tf_op jit(solution)/shard_map/add | solution.py:58
  107.8 6.6 %fusion.29 = f32[256,24]{0,1:T(8,128)S(1)} fusion(f32[24,4,2048]{2,0,1:T(8,128)S(1)} %all_gather.7, f32[256,1,2048]{2,0,1:T(8,128)S(1)} %bitcast.111, f32[256,1,2048]{2,0,1:T(8,128)S(1)} %bitcast.108, f32[256,1,2048]{2,0,1:T(8,128)S(1)} %bitcast.105, f32[256,1,2048]{2,0,1:T(8,128)S(1)} %bitcast.102), kind=kOutput, calls=%fused_computation.55 | convolution fusion | flops 610271232 | bytes 9199616 | tf_op jit(solution)/shard_map/tic,kic->tk/dot_general | solution.py:95
  114.4 0.9 multiply_reduce_fusion
  115.3 10.8 %psum.22 = f32[256,25]{0,1:T(8,128)S(1)} all-reduce(f32[256,25]{0,1:T(8,128)S(1)} %pad_maximum_fusion.4), channel_id=1, replica_groups=mesh['dp'=8,'mp'=4] {'mp'}, use_global_device_ids=true, to_apply=%region_15.16 | all-reduce | flops 6400 | bytes 51200 | tf_op jit(solution)/shard_map/psum | solution.py:20
  126.1 1.4 fusion.45
  127.5 0.6 slice_multiply_fusion
  128.1 0.1 fusion.72
  128.2 0.1 divide_reduce_fusion
  128.3 0.1 divide_reduce_fusion.6
  128.4 0.1 divide_reduce_fusion.5
  128.5 0.1 divide_reduce_fusion.4
  128.7 0.1 divide_reduce_fusion.3
  128.8 0.1 divide_reduce_fusion.2
  128.9 0.7 exponential_divide_fusion
  129.6 0.6 pad_maximum_fusion.6
  130.2 4.9 %multiply_reduce_fusion.1 = (f32[256]{0:T(256)S(1)}, f32[256,2048]{1,0:T(8,128)}) fusion(f32[256,2048]{1,0:T(8,128)} %copy-done.3, f32[256]{0:T(256)S(1)} %bitcast.143, f32[256,2048]{1,0:T(8,128)} %copy-done.2, f32[256]{0:T(256)S(1)} %bitcast.144, f32[256,2048]{1,0:T(8,128)} %copy-done, f32[256]{0:T(256)S(1)} %bitcast.145, ...), kind=kLoop, calls=%fused_computation.49 | loop fusion | flops 4718336 | bytes 10490880 | tf_op jit(solution)/shard_map/reduce_sum | solution.py:111
  135.1 5.9 %psum.23 = f32[256]{0:T(256)S(1)} all-reduce(f32[256]{0:T(256)S(1)} %get-tuple-element.6), channel_id=1, replica_groups=mesh['dp'=8,'mp'=4] {'mp'}, use_global_device_ids=true, to_apply=%region_17.18 | all-reduce | flops 256 | bytes 2048 | tf_op jit(solution)/shard_map/psum | solution.py:111
  141.1 3.0 %multiply_convert_fusion = bf16[256,2048]{1,0:T(8,128)(2,1)} fusion(f32[256,2048]{1,0:T(8,128)} %get-tuple-element.7, f32[2048]{0:T(1024)S(1)} %copy-done.9, f32[256]{0:T(256)S(1)} %add_sqrt_fusion), kind=kLoop, calls=%fused_computation.48 | loop fusion | flops 1572864 | bytes 3154944 | tf_op jit(solution)/shard_map/convert_element_type | solution.py:112
  144.1 2.6 %fusion.27 = bf16[256,4,2048]{2,0,1:T(8,128)(2,1)S(1)} fusion(f32[256,1,2048]{2,0,1:T(8,128)} %bitcast.113, f32[256,1,2048]{2,0,1:T(8,128)} %bitcast.110, f32[256,1,2048]{2,0,1:T(8,128)S(1)} %bitcast.107, f32[256,1,2048]{2,0,1:T(8,128)S(1)} %bitcast.104), kind=kLoop, calls=%fused_computation.52 | loop fusion | flops 6291456 | bytes 12582912 | tf_op jit(solution)/shard_map/convert_element_type | solution.py:94
  146.7 5.3 %copy.17 = bf16[256,4,2048]{2,1,0:T(4,128)(2,1)} copy(bf16[256,4,2048]{2,0,1:T(8,128)(2,1)S(1)} %fusion.27) | data formatting | bytes 8388608
  (49 shorter events, 0.7 us)
Async XLA Ops:
  0.6 9.4 %copy-start.7 = (f32[44]{0:T(128)S(1)}, f32[44]{0:T(128)}, u32[]{:S(2)}) copy-start(f32[44]{0:T(128)} %param.11) | copy-start | bytes 532
  0.7 9.8 %copy-start.8 = (f32[5]{0:T(128)S(1)}, f32[5]{0:T(128)}, u32[]{:S(2)}) copy-start(f32[5]{0:T(128)} %param.12) | copy-start | bytes 64
  0.7 10.4 %copy-start.6 = (f32[20,4,256]{2,1,0:T(4,128)S(1)}, f32[20,4,256]{2,1,0:T(4,128)}, u32[]{:S(2)}) copy-start(f32[20,4,256]{2,1,0:T(4,128)} %param.9) | copy-start | bytes 245764
  0.7 10.4 %copy-start.5 = (f32[24,4,256]{2,1,0:T(4,128)S(1)}, f32[24,4,256]{2,1,0:T(4,128)}, u32[]{:S(2)}) copy-start(f32[24,4,256]{2,1,0:T(4,128)} %param.10) | copy-start | bytes 294916
  98.6 4.6 %copy-start.4 = (bf16[256,2048]{1,0:T(8,128)(2,1)S(1)}, bf16[256,2048]{1,0:T(8,128)(2,1)}, u32[]{:S(2)}) copy-start(bf16[256,2048]{1,0:T(8,128)(2,1)} %param.8) | copy-start | bytes 3145732
  105.5 8.9 %copy-start = (f32[256,2048]{1,0:T(8,128)}, f32[256,2048]{1,0:T(8,128)S(1)}, u32[]{:S(2)}) copy-start(f32[256,2048]{1,0:T(8,128)S(1)} %get-tuple-element.11) | copy-start | bytes 6291460
  107.8 6.6 %copy-start.2 = (f32[256,2048]{1,0:T(8,128)}, f32[256,2048]{1,0:T(8,128)S(1)}, u32[]{:S(2)}) copy-start(f32[256,2048]{1,0:T(8,128)S(1)} %get-tuple-element.12) | copy-start | bytes 6291460
  107.8 6.6 %copy-start.3 = (f32[256,2048]{1,0:T(8,128)}, f32[256,2048]{1,0:T(8,128)S(1)}, u32[]{:S(2)}) copy-start(f32[256,2048]{1,0:T(8,128)S(1)} %get-tuple-element.13) | copy-start | bytes 6291460
  130.2 10.8 %copy-start.9 = (f32[2048]{0:T(1024)S(1)}, f32[2048]{0:T(1024)}, u32[]{:S(2)}) copy-start(f32[2048]{0:T(1024)} %param.13) | copy-start | bytes 24580
  141.0 3.1 %copy-start.1 = (f32[256,2048]{1,0:T(8,128)S(1)}, f32[256,2048]{1,0:T(8,128)}, u32[]{:S(2)}) copy-start(f32[256,2048]{1,0:T(8,128)} %copy-done) | copy-start | bytes 6291460
where the time goes:
time: 152 us
  blocking collectives  93.1 us (61%)
  matrix products  25.2 us (17%)
  other arithmetic  21.8 us (14%)
  local copies, waits for them, and re-layouts  10.9 us (7%)
    all_gather x1, blocking collectives, local(): lax.all_gather(next_weight, 'dp', axis=2, tiled=True)  33.9 us
    all_gather x1, blocking collectives, local(): lax.all_gather(merge_weight, 'dp', axis=2, tiled=True)  32.1 us
    psum x2, blocking collectives, settle(): summed = lax.psum(columns, 'mp')  21.2 us
    unnamed x26, local copies, waits for them, and re-layouts  9.92 us
    dot_general x1, matrix products, local(): jnp.einsum('tic,tjc->tij', streams, streams, preferred_element_type=jnp.f...  9.4 us
    dot_general x1, matrix products, local(): jnp.einsum('tic,kic->tk', streams, merge_rows, precision=highest, preferr...  9.18 us
    dot_general x1, matrix products, local(): raw_next = jnp.einsum('tic,kic->tk', mixed, next_rows, precision=highest)  6.59 us
    psum x1, blocking collectives, local(): united_sq = lax.psum(jnp.sum(united * united, axis=1), 'mp')  5.92 us

commit v1 on v0

--- a/solution.py
+++ b/solution.py
@@ -17,7 +17,7 @@
 
 
 def settle(columns, finish):
-    summed = lax.psum(columns, "mp")
+    summed = lax.all_gather(columns, axis_name="mp").sum(axis=0)
     result = finish(summed)
     return result
 

time: 152 us -> 144 us (0.947)
  blocking collectives: 93.1 us -> 84.2 us
    psum x2 -> x0, blocking collectives: 21.2 us -> none  [settle(): summed = lax.psum(columns, 'mp')]
    all_gather x0 -> x2, blocking collectives: none -> 11.1 us  [settle(): summed = lax.all_gather(columns, axis_name='mp').sum(axis=0)]
where the time goes in v1:
time: 144 us; the launch traced here: 143 us
  blocking collectives  84.2 us (58%)
  matrix products  25.2 us (18%)
  other arithmetic  21.9 us (15%)
  local copies, waits for them, and re-layouts  11 us (8%)
    all_gather x1, blocking collectives, local(): lax.all_gather(next_weight, 'dp', axis=2, tiled=True)  33.9 us
    all_gather x1, blocking collectives, local(): lax.all_gather(merge_weight, 'dp', axis=2, tiled=True)  32.1 us
    all_gather x2, blocking collectives, settle(): summed = lax.all_gather(columns, axis_name='mp').sum(axis=0)  11.1 us
    unnamed x26, local copies, waits for them, and re-layouts  9.92 us
    dot_general x1, matrix products, local(): jnp.einsum('tic,tjc->tij', streams, streams, preferred_element_type=jnp.f...  9.4 us
    dot_general x1, matrix products, local(): jnp.einsum('tic,kic->tk', streams, merge_rows, precision=highest, preferr...  9.18 us
    psum x1, blocking collectives, local(): united_sq = lax.psum(jnp.sum(united * united, axis=1), 'mp')  7.06 us
    dot_general x1, matrix products, local(): raw_next = jnp.einsum('tic,kic->tk', mixed, next_rows, precision=highest)  6.59 us

profile of v1, /device:TPU:0, one launch (start us, length us, event | category | flops | bytes accessed | tf_op | source)
XLA Modules:
  0.0 143.3 jit_solution(17689342849189123458)
XLA Ops:
  0.7 9.4 %fusion.28 = f32[256]{0:T(256)S(1)} fusion(bf16[256,4,2048]{2,1,0:T(4,128)(2,1)} %param.7, pred[4,4]{1,0:T(4,128)(4,1)S(1)} %iota_compare_fusion), kind=kOutput, calls=%fused_computation.54 | convolution fusion | flops 16785152 | bytes 4195344 | tf_op jit(solution)/shard_map/tic,tjc->tij/dot_general | solution.py:81
  10.2 0.1 add.132
  10.4 0.6 fusion.78
  11.1 33.9 %all_gather.21 = f32[24,4,2048]{2,0,1:T(8,128)S(1)} all-gather(f32[24,4,256]{2,0,1:T(8,128)S(1)} %copy.16), channel_id=1, replica_groups=mesh['dp'=8,'mp'=4] {'dp'}, dimensions={2}, use_global_device_ids=true | all-gather | bytes 884736 | tf_op jit(solution)/shard_map/all_gather | solution.py:75
  45.0 32.1 %all_gather.18 = f32[20,4,2048]{2,0,1:T(8,128)S(1)} all-gather(f32[20,4,256]{2,0,1:T(8,128)S(1)} %copy.10), channel_id=1, replica_groups=mesh['dp'=8,'mp'=4] {'dp'}, dimensions={2}, use_global_device_ids=true | all-gather | bytes 737280 | tf_op jit(solution)/shard_map/all_gather | solution.py:74
  77.1 9.2 %convolution_bitcast_fusion = f32[256,20]{0,1:T(8,128)S(1)} fusion(f32[20,4,2048]{2,0,1:T(8,128)S(1)} %all_gather.18, bf16[256,4,2048]{2,1,0:T(4,128)(2,1)} %param.7), kind=kOutput, calls=%fused_computation.56 | convolution fusion | flops 503316480 | bytes 4870144 | tf_op jit(solution)/shard_map/tic,kic->tk/dot_general | solution.py:78
  86.3 5.5 %all-gather = f32[1024,21]{0,1:T(8,128)S(1)} all-gather(f32[256,21]{0,1:T(8,128)S(1)} %pad_maximum_fusion.5), channel_id=2, replica_groups=mesh['dp'=8,'mp'=4] {'mp'}, dimensions={0}, use_global_device_ids=true | all-gather | bytes 107520 | tf_op jit(solution)/shard_map/all_gather | solution.py:20
  91.9 0.8 fusion.56
  92.7 0.7 slice_multiply_fusion.1
  93.4 0.1 fusion.74
  93.8 4.6 %copy.11 = bf16[256,4,2048]{2,0,1:T(8,128)(2,1)S(1)} copy(bf16[256,4,2048]{2,1,0:T(4,128)(2,1)} %param.7) | data formatting | bytes 8388608 | tf_op args[0]
  98.4 2.3 %fusion.13 = (f32[256,2048]{1,0:T(8,128)S(1)}, f32[256,2048]{1,0:T(8,128)S(1)}) fusion(bf16[256,2048]{1,0:T(8,128)(2,1)S(1)} %copy-done.4, f32[256]{0:T(256)S(1)} %bitcast.139, f32[256]{0:T(256)S(1)} %bitcast.140, f32[256]{0:T(256)S(1)} %bitcast.141, f32[256]{0:T(256)S(1)} %bitcast.134, f32[256]{0:T(256)S(1)} %bitcast.144, ...), kind=kLoop, calls=%fused_computation.35 | loop fusion | flops 12058624 | bytes 9447424 | tf_op jit(solution)/shard_map/add | solution.py:58
  100.6 2.3 %fusion.21 = (f32[256,2048]{1,0:T(8,128)S(1)}, f32[256,2048]{1,0:T(8,128)S(1)}) fusion(bf16[256,2048]{1,0:T(8,128)(2,1)S(1)} %copy-done.4, f32[256]{0:T(256)S(1)} %bitcast.130, f32[256]{0:T(256)S(1)} %bitcast.131, f32[256]{0:T(256)S(1)} %bitcast.132, f32[256]{0:T(256)S(1)} %bitcast.133, f32[256]{0:T(256)S(1)} %bitcast.143, ...), kind=kLoop, calls=%fused_computation.43 | loop fusion | flops 12058624 | bytes 9447424 | tf_op jit(solution)/shard_map/add | solution.py:58
  103.0 6.6 %fusion.29 = f32[256,24]{0,1:T(8,128)S(1)} fusion(f32[24,4,2048]{2,0,1:T(8,128)S(1)} %all_gather.21, f32[256,1,2048]{2,0,1:T(8,128)S(1)} %bitcast.115, f32[256,1,2048]{2,0,1:T(8,128)S(1)} %bitcast.112, f32[256,1,2048]{2,0,1:T(8,128)S(1)} %bitcast.109, f32[256,1,2048]{2,0,1:T(8,128)S(1)} %bitcast.106), kind=kOutput, calls=%fused_computation.55 | convolution fusion | flops 610271232 | bytes 9199616 | tf_op jit(solution)/shard_map/tic,kic->tk/dot_general | solution.py:95
  109.6 0.9 multiply_reduce_fusion
  110.5 5.6 %all-gather.1 = f32[1024,25]{0,1:T(8,128)S(1)} all-gather(f32[256,25]{0,1:T(8,128)S(1)} %pad_maximum_fusion.4), channel_id=3, replica_groups=mesh['dp'=8,'mp'=4] {'mp'}, dimensions={0}, use_global_device_ids=true | all-gather | bytes 128000 | tf_op jit(solution)/shard_map/all_gather | solution.py:20
  116.3 1.4 fusion.45
  117.7 0.6 slice_multiply_fusion
  118.3 0.1 fusion.72
  118.4 0.1 divide_reduce_fusion
  118.5 0.1 divide_reduce_fusion.6
  118.6 0.1 divide_reduce_fusion.5
  118.7 0.1 divide_reduce_fusion.4
  118.8 0.1 divide_reduce_fusion.3
  118.9 0.1 divide_reduce_fusion.2
  119.1 0.7 exponential_divide_fusion
  119.8 0.6 pad_maximum_fusion.6
  120.4 4.9 %multiply_reduce_fusion.1 = (f32[256]{0:T(256)S(1)}, f32[256,2048]{1,0:T(8,128)}) fusion(f32[256,2048]{1,0:T(8,128)} %copy-done.3, f32[256]{0:T(256)S(1)} %bitcast.147, f32[256,2048]{1,0:T(8,128)} %copy-done.2, f32[256]{0:T(256)S(1)} %bitcast.148, f32[256,2048]{1,0:T(8,128)} %copy-done, f32[256]{0:T(256)S(1)} %bitcast.149, ...), kind=kLoop, calls=%fused_computation.49 | loop fusion | flops 4718336 | bytes 10490880 | tf_op jit(solution)/shard_map/reduce_sum | solution.py:111
  125.3 7.1 %psum.7 = f32[256]{0:T(256)S(1)} all-reduce(f32[256]{0:T(256)S(1)} %get-tuple-element.6), channel_id=1, replica_groups=mesh['dp'=8,'mp'=4] {'mp'}, use_global_device_ids=true, to_apply=%region_17.18 | all-reduce | flops 256 | bytes 2048 | tf_op jit(solution)/shard_map/psum | solution.py:111
  132.4 3.0 %multiply_convert_fusion = bf16[256,2048]{1,0:T(8,128)(2,1)} fusion(f32[256,2048]{1,0:T(8,128)} %get-tuple-element.7, f32[2048]{0:T(1024)S(1)} %copy-done.9, f32[256]{0:T(256)S(1)} %add_sqrt_fusion), kind=kLoop, calls=%fused_computation.48 | loop fusion | flops 1572864 | bytes 3154944 | tf_op jit(solution)/shard_map/convert_element_type | solution.py:112
  135.4 2.6 %fusion.27 = bf16[256,4,2048]{2,0,1:T(8,128)(2,1)S(1)} fusion(f32[256,1,2048]{2,0,1:T(8,128)} %bitcast.117, f32[256,1,2048]{2,0,1:T(8,128)} %bitcast.114, f32[256,1,2048]{2,0,1:T(8,128)S(1)} %bitcast.111, f32[256,1,2048]{2,0,1:T(8,128)S(1)} %bitcast.108), kind=kLoop, calls=%fused_computation.52 | loop fusion | flops 6291456 | bytes 12582912 | tf_op jit(solution)/shard_map/convert_element_type | solution.py:94
  138.0 5.3 %copy.17 = bf16[256,4,2048]{2,1,0:T(4,128)(2,1)} copy(bf16[256,4,2048]{2,0,1:T(8,128)(2,1)S(1)} %fusion.27) | data formatting | bytes 8388608
  (53 shorter events, 0.9 us)
Async XLA Ops:
  0.6 9.4 %copy-start.7 = (f32[44]{0:T(128)S(1)}, f32[44]{0:T(128)}, u32[]{:S(2)}) copy-start(f32[44]{0:T(128)} %param.11) | copy-start | bytes 532
  0.7 9.8 %copy-start.8 = (f32[5]{0:T(128)S(1)}, f32[5]{0:T(128)}, u32[]{:S(2)}) copy-start(f32[5]{0:T(128)} %param.12) | copy-start | bytes 64
  0.7 10.4 %copy-start.6 = (f32[20,4,256]{2,1,0:T(4,128)S(1)}, f32[20,4,256]{2,1,0:T(4,128)}, u32[]{:S(2)}) copy-start(f32[20,4,256]{2,1,0:T(4,128)} %param.9) | copy-start | bytes 245764
  0.7 10.4 %copy-start.5 = (f32[24,4,256]{2,1,0:T(4,128)S(1)}, f32[24,4,256]{2,1,0:T(4,128)}, u32[]{:S(2)}) copy-start(f32[24,4,256]{2,1,0:T(4,128)} %param.10) | copy-start | bytes 294916
  93.8 4.6 %copy-start.4 = (bf16[256,2048]{1,0:T(8,128)(2,1)S(1)}, bf16[256,2048]{1,0:T(8,128)(2,1)}, u32[]{:S(2)}) copy-start(bf16[256,2048]{1,0:T(8,128)(2,1)} %param.8) | copy-start | bytes 3145732
  100.6 8.9 %copy-start = (f32[256,2048]{1,0:T(8,128)}, f32[256,2048]{1,0:T(8,128)S(1)}, u32[]{:S(2)}) copy-start(f32[256,2048]{1,0:T(8,128)S(1)} %get-tuple-element.11) | copy-start | bytes 6291460
  102.9 6.6 %copy-start.2 = (f32[256,2048]{1,0:T(8,128)}, f32[256,2048]{1,0:T(8,128)S(1)}, u32[]{:S(2)}) copy-start(f32[256,2048]{1,0:T(8,128)S(1)} %get-tuple-element.12) | copy-start | bytes 6291460
  102.9 6.6 %copy-start.3 = (f32[256,2048]{1,0:T(8,128)}, f32[256,2048]{1,0:T(8,128)S(1)}, u32[]{:S(2)}) copy-start(f32[256,2048]{1,0:T(8,128)S(1)} %get-tuple-element.13) | copy-start | bytes 6291460
  120.4 12.0 %copy-start.9 = (f32[2048]{0:T(1024)S(1)}, f32[2048]{0:T(1024)}, u32[]{:S(2)}) copy-start(f32[2048]{0:T(1024)} %param.13) | copy-start | bytes 24580
  132.3 3.1 %copy-start.1 = (f32[256,2048]{1,0:T(8,128)S(1)}, f32[256,2048]{1,0:T(8,128)}, u32[]{:S(2)}) copy-start(f32[256,2048]{1,0:T(8,128)} %copy-done) | copy-start | bytes 6291460
